TPU v7x, 128 devices: a whole 4x4x4 slice. The times are simulated.
128 devices in a mesh: ctx: 16 (over z, x_lo, core), tp: 8 (over x_hi, y).
Axes of the slice: x: 4 (x_hi: 2, x_lo: 2; x = x_hi * 2 + x_lo), y: 4, z: 4, core: 2. Of those that a mesh axis runs over, the one named last changes fastest.
Arguments:
- tokens: bfloat16 [2, 4096, 8192], P(None, 'ctx', 'tp'), may hold values from -14 to 14
- norm_gain: float32 [8192], replicated, may hold values from 0.5 to 1.5
- span_order: int32 [2, 32], replicated, may hold values from 0 to 31, each once within a row
- w_query: bfloat16 [8192, 4096], P('ctx', 'tp'), may hold values from -0.10122281 to 0.10122281
- w_key: bfloat16 [8192, 1024], P('ctx', 'tp'), may hold values from -0.10122281 to 0.10122281
- value_weight: bfloat16 [8192, 1024], P('ctx', 'tp'), may hold values from -0.0625 to 0.0625
- w_out: bfloat16 [4096, 8192], P('tp', 'ctx'), may hold values from -0.75 to 0.75
Outputs:
- mixed: bfloat16 [2, 4096, 8192], P(None, 'ctx', 'tp')
Inputs may be any that keep to these rules, and one draw needn't show every extreme that they name: Each row of span_order names every one of the 2 * 16 blocks of positions once; stored block b of a sequence holds positions span_order[b] * 128 onwards, in order.
All inputs are finite; a program needn't handle non-finite values.
Results may differ from a plain program's by a relative error of at most 0.014.
Values may be sent and summed in bfloat16 or wider, within the bound.
A program may use at most 128 MiB of HBM per device.

v0:
```python
import math
import jax
import jax.numpy as jnp
from jax import lax
from jax.sharding import PartitionSpec as P

HEAD_DIM = 128
theta_base = 500000.0
norm_eps = 1e-05
masked_score = -1e30


def in_one_piece(arrays, axis, dim, along):
    ends, at = ([], 0)
    for a in arrays[:-1]:
        at += a.shape[along]
        ends.append(at)
    both = jnp.concatenate(arrays, axis=along)
    return tuple(jnp.split(lax.all_gather(both, axis, axis=dim, tiled=True), ends, axis=along))


def normalize(flat_rows, norm_gain):
    wide = flat_rows.astype(jnp.float32)
    factor = lax.rsqrt(jnp.mean(wide * wide, axis=-1, keepdims=True) + norm_eps)
    return (wide * factor * norm_gain).astype(jnp.bfloat16)


def positions_of(span_order, first, count, block_rows):
    stored = first + jnp.arange(count, dtype=jnp.int32)
    which = stored // block_rows
    slots = jnp.arange(span_order.shape[1], dtype=jnp.int32)
    picked = jnp.sum(
        jnp.where(slots[None, None, :] == which[None, :, None], span_order[:, None, :], 0), axis=2
    )
    return picked * block_rows + stored % block_rows


def apply_rotation(value_rows, token_position, head_size):
    half = head_size // 2
    freqs = jnp.exp(-(2.0 * jnp.arange(half, dtype=jnp.float32) / head_size) * math.log(theta_base))
    angle = token_position.astype(jnp.float32)[..., None] * freqs
    cosine = jnp.cos(angle)[:, :, None, :]
    sine = jnp.sin(angle)[:, :, None, :]
    front = value_rows[..., :half]
    back = value_rows[..., half:]
    return jnp.concatenate([front * cosine - back * sine, back * cosine + front * sine], axis=-1)


def per_device(tokens, norm_gain, span_order, w_query, w_key, value_weight, w_out):
    sequence_batch, rows_dev, _ = tokens.shape
    head_size = HEAD_DIM
    query_heads = w_query.shape[1] // head_size
    key_heads = w_key.shape[1] // head_size
    group_width = query_heads // key_heads
    block_rows = rows_dev // 2
    total_rows = sequence_batch * rows_dev
    factor = 1.0 / math.sqrt(head_size)
    rank = lax.axis_index("ctx")
    whole = lax.all_gather(tokens, "tp", axis=2, tiled=True)
    normed = normalize(whole.reshape(total_rows, whole.shape[2]), norm_gain)
    query_pos = positions_of(span_order, rank * rows_dev, rows_dev, block_rows)
    latest = jnp.max(query_pos, axis=1)
    stat_shape = (sequence_batch, key_heads, group_width, rows_dev)
    initial = (
        jnp.full(stat_shape, masked_score, jnp.float32),
        jnp.zeros(stat_shape, jnp.float32),
        jnp.zeros(stat_shape + (head_size,), jnp.float32),
    )
    pieces = in_one_piece((w_query, w_key, value_weight), "ctx", 0, 1)
    query_flat, flattened_key, flattened_value = tuple(
        (jnp.dot(normed, piece, preferred_element_type=jnp.float32) for piece in pieces)
    )
    turned = apply_rotation(
        query_flat.reshape(sequence_batch, rows_dev, query_heads, head_size), query_pos, head_size
    ).astype(jnp.bfloat16)
    query = turned.reshape(sequence_batch, rows_dev, key_heads, group_width, head_size).transpose(
        0, 2, 3, 1, 4
    )
    turned = apply_rotation(
        flattened_key.reshape(sequence_batch, rows_dev, key_heads, head_size), query_pos, head_size
    ).astype(jnp.bfloat16)
    own_values = flattened_value.reshape(sequence_batch, rows_dev, key_heads, head_size).astype(
        jnp.bfloat16
    )
    key_piece, value_piece = in_one_piece((turned, own_values), "ctx", 1, 0)
    count = key_piece.shape[1]
    step_rows = 512

    def one_block(index, state):
        first = index * step_rows
        key_block = lax.dynamic_slice_in_dim(key_piece, first, step_rows, 1)
        value_block = lax.dynamic_slice_in_dim(value_piece, first, step_rows, 1)
        key_pos = positions_of(span_order, first, step_rows, block_rows)

        def update(current):
            peak, total, summed = current
            scores = (
                jnp.einsum(
                    "shgqd,skhd->shgqk", query, key_block, preferred_element_type=jnp.float32
                )
                * factor
            )
            allowed = key_pos[:, None, None, None, :] <= query_pos[:, None, None, :, None]
            scores = jnp.where(allowed, scores, masked_score)
            new_peak = jnp.maximum(peak, jnp.max(scores, axis=-1))
            weights = jnp.where(allowed, jnp.exp(scores - new_peak[..., None]), 0.0)
            shrink = jnp.exp(peak - new_peak)
            total = total * shrink + jnp.sum(weights, axis=-1)
            summed = summed * shrink[..., None] + jnp.einsum(
                "shgqk,skhd->shgqd",
                weights.astype(jnp.bfloat16),
                value_block,
                preferred_element_type=jnp.float32,
            )
            return (new_peak, total, summed)

        return lax.cond(
            jnp.all(jnp.min(key_pos, axis=1) > latest), lambda kept: kept, update, state
        )

    peak, total, summed = lax.fori_loop(0, count // step_rows, one_block, initial)
    attended = (summed / total[..., None]).astype(jnp.bfloat16)
    attended = attended.transpose(0, 3, 1, 2, 4).reshape(total_rows, query_heads * head_size)
    terms = jnp.dot(
        attended,
        lax.all_gather(w_out, "ctx", axis=1, tiled=True),
        preferred_element_type=jnp.float32,
    )
    mixed = lax.psum_scatter(terms.astype(jnp.bfloat16), "tp", scatter_dimension=1, tiled=True)
    return mixed.reshape(sequence_batch, rows_dev, mixed.shape[1])


def solution(mesh):
    placed = (
        P(None, "ctx", "tp"),
        P(),
        P(),
        P("ctx", "tp"),
        P("ctx", "tp"),
        P("ctx", "tp"),
        P("tp", "ctx"),
    )
    return jax.shard_map(
        per_device, mesh=mesh, in_specs=placed, out_specs=P(None, "ctx", "tp"), check_vma=False
    )
```

profile of v0, /device:TPU:0, one launch (start us, length us, event | category | flops | bytes accessed | tf_op | source)
XLA Modules:
  0.0 453.7 jit_solution(2648720766434171846)
XLA Ops:
  11.8 106.8 %all-gather.5.cloned.1.call-done = bf16[2,256,8192]{2,1,0:T(8,128)(2,1)} async-done(((bf16[2,256,1024]{2,1,0:T(8,128)(2,1)}), bf16[2,256,8192]{2,1,0:T(8,128)(2,1)}) %all-gather.5.cloned.1.call-update) | async-done | bytes 8388624 | tf_op jit(solution)/shard_map/all_gather | solution.py:59
  118.6 5.1 %fusion.27 = f32[2,256]{1,0:T(2,128)S(1)} fusion(bf16[2,256,8192]{2,1,0:T(8,128)(2,1)} %all-gather.5.cloned.1.call-done), kind=kLoop, calls=%fused_computation.41 | loop fusion | flops 12582400 | bytes 8390656 | tf_op jit(solution)/shard_map/reduce_sum | solution.py:24
  123.7 66.3 %all-gather.7.cloned.1.call-done = bf16[8192,768]{0,1:T(8,128)(2,1)} async-done(((bf16[512,768]{0,1:T(8,128)(2,1)}), bf16[8192,768]{0,1:T(8,128)(2,1)}) %all-gather.7.cloned.1.call-update) | async-done | bytes 12582928 | tf_op jit(solution)/shard_map/all_gather | solution.py:19
  190.0 7.0 %fusion.37 = f32[2,256,1,128]{1,3,0,2:T(8,128)S(1)} fusion(bf16[8192,768]{0,1:T(8,128)(2,1)} %all-gather.7.cloned.1.call-done, bf16[2,256,8192]{2,1,0:T(8,128)(2,1)} %all-gather.5.cloned.1.call-done, f32[8192]{0:T(1024)S(1)} %copy-done.1, f32[2,256]{1,0:T(2,128)S(1)} %add_rsqrt_fusion), kind=kOutput, calls=%fused_computation.51 | convolution fusion | flops 1090519040 | bytes 10782720 | tf_op jit(solution)/shard_map/dot_general | solution.py:71
  197.6 7.0 %fusion.43 = bf16[2,256,1,128]{1,3,0,2:T(8,128)(2,1)S(1)} fusion(bf16[8192,768]{0,1:T(8,128)(2,1)} %all-gather.7.cloned.1.call-done, bf16[2,256,8192]{2,1,0:T(8,128)(2,1)} %all-gather.5.cloned.1.call-done, f32[8192]{0:T(1024)S(1)} %copy-done.1, f32[2,256]{1,0:T(2,128)S(1)} %add_rsqrt_fusion), kind=kOutput, calls=%fused_computation.53 | convolution fusion | flops 1090584576 | bytes 10651648 | tf_op jit(solution)/shard_map/dot_general | solution.py:71
  206.8 7.7 %split.23 = bf16[8192,512]{0,1:T(8,128)(2,1)} slice(bf16[8192,768]{0,1:T(8,128)(2,1)} %all-gather.7.cloned.1.call-done), slice={[0:8192], [0:512]} | slice | bytes 16777216 | tf_op jit(solution)/shard_map/split | solution.py:19
  214.6 9.8 %fusion.30 = f32[2,256,4,128]{1,3,2,0:T(8,128)S(1)} fusion(bf16[4,128,8192,1]{2,1,0,3:T(8,128)(2,1)} %bitcast.90, bf16[2,256,8192]{2,1,0:T(8,128)(2,1)} %all-gather.5.cloned.1.call-done, f32[8192]{0:T(1024)S(1)} %copy-done.1, f32[2,256]{1,0:T(2,128)S(1)} %add_rsqrt_fusion), kind=kOutput, calls=%fused_computation.45 | convolution fusion | flops 4311744512 | bytes 17860608 | tf_op jit(solution)/shard_map/dot_general | solution.py:71
  224.8 26.8 %all-gather.9.cloned.1.call-done = bf16[4,4096,1,128]{1,3,0,2:T(8,128)(2,1)} async-done(((bf16[4,256,1,128]{1,3,0,2:T(8,128)(2,1)}), bf16[4,4096,1,128]{1,3,0,2:T(8,128)(2,1)}) %all-gather.9.cloned.1.call-update) | async-done | bytes 4194320 | tf_op jit(solution)/shard_map/all_gather | solution.py:19
  251.6 3.9 fusion.62
  255.5 4.1 copy.33
  259.6 2.4 copy.35
  262.1 59.5 %while.19 = (s32[]{:T(128)}, f32[2,1,4,256]{3,2,0,1:T(4,128)S(1)}, f32[2,1,4,256]{3,2,0,1:T(4,128)S(1)}, f32[2,1,4,256,128]{4,3,2,0,1:T(8,128)S(1)}, s32[2,32]{1...) while((s32[]{:T(128)}, f32[2,1,4,256]{3,2,0,1:T(4,128)S(1)}, ...), condition=%wide.region_11.12_spmd, body=%wide.region_3.11_spmd.sunk | while | flops 551389184 | bytes 16968260 | solution.py:121
  263.8 5.7 %conditional.2 = (f32[2,1,4,256]{3,2,0,1:T(4,128)S(1)}, f32[2,1,4,256]{3,2,0,1:T(4,128)S(1)}, f32[2,1,4,256,128]{4,3,2,0,1:T(8,128)S(1)}) conditional(s32[]{:T(128)} %convert_element_type.120, (s32[2,512]{1,0:T(2,128)S(1)}, s32[2,256]{1,0:T(2,128)S(1)}, s32[]{:T(128)}, bf16[2,4096,1,128]{3,1,0,2:T(8,128)(2,1)}, ...), branch_computations={%region_7.9_spmd, %region_10.10_spmd} | conditional | flops 551294976 | bytes 16898114 | solution.py:117
  265.8 2.6 fusion.9
  271.2 5.8 %conditional.2 = (f32[2,1,4,256]{3,2,0,1:T(4,128)S(1)}, f32[2,1,4,256]{3,2,0,1:T(4,128)S(1)}, f32[2,1,4,256,128]{4,3,2,0,1:T(8,128)S(1)}) conditional(s32[]{:T(128)} %convert_element_type.120, (s32[2,512]{1,0:T(2,128)S(1)}, s32[2,256]{1,0:T(2,128)S(1)}, s32[]{:T(128)}, bf16[2,4096,1,128]{3,1,0,2:T(8,128)(2,1)}, ...), branch_computations={%region_7.9_spmd, %region_10.10_spmd} | conditional | flops 551294976 | bytes 16898114 | solution.py:117
  271.4 1.8 fusion
  273.2 2.6 fusion.9
  278.6 5.8 %conditional.2 = (f32[2,1,4,256]{3,2,0,1:T(4,128)S(1)}, f32[2,1,4,256]{3,2,0,1:T(4,128)S(1)}, f32[2,1,4,256,128]{4,3,2,0,1:T(8,128)S(1)}) conditional(s32[]{:T(128)} %convert_element_type.120, (s32[2,512]{1,0:T(2,128)S(1)}, s32[2,256]{1,0:T(2,128)S(1)}, s32[]{:T(128)}, bf16[2,4096,1,128]{3,1,0,2:T(8,128)(2,1)}, ...), branch_computations={%region_7.9_spmd, %region_10.10_spmd} | conditional | flops 551294976 | bytes 16898114 | solution.py:117
  280.7 2.7 fusion.9
  286.1 5.8 %conditional.2 = (f32[2,1,4,256]{3,2,0,1:T(4,128)S(1)}, f32[2,1,4,256]{3,2,0,1:T(4,128)S(1)}, f32[2,1,4,256,128]{4,3,2,0,1:T(8,128)S(1)}) conditional(s32[]{:T(128)} %convert_element_type.120, (s32[2,512]{1,0:T(2,128)S(1)}, s32[2,256]{1,0:T(2,128)S(1)}, s32[]{:T(128)}, bf16[2,4096,1,128]{3,1,0,2:T(8,128)(2,1)}, ...), branch_computations={%region_7.9_spmd, %region_10.10_spmd} | conditional | flops 551294976 | bytes 16898114 | solution.py:117
  288.1 2.6 fusion.9
  293.5 5.8 %conditional.2 = (f32[2,1,4,256]{3,2,0,1:T(4,128)S(1)}, f32[2,1,4,256]{3,2,0,1:T(4,128)S(1)}, f32[2,1,4,256,128]{4,3,2,0,1:T(8,128)S(1)}) conditional(s32[]{:T(128)} %convert_element_type.120, (s32[2,512]{1,0:T(2,128)S(1)}, s32[2,256]{1,0:T(2,128)S(1)}, s32[]{:T(128)}, bf16[2,4096,1,128]{3,1,0,2:T(8,128)(2,1)}, ...), branch_computations={%region_7.9_spmd, %region_10.10_spmd} | conditional | flops 551294976 | bytes 16898114 | solution.py:117
  293.8 1.8 fusion
  295.6 2.6 fusion.9
  301.0 5.8 %conditional.2 = (f32[2,1,4,256]{3,2,0,1:T(4,128)S(1)}, f32[2,1,4,256]{3,2,0,1:T(4,128)S(1)}, f32[2,1,4,256,128]{4,3,2,0,1:T(8,128)S(1)}) conditional(s32[]{:T(128)} %convert_element_type.120, (s32[2,512]{1,0:T(2,128)S(1)}, s32[2,256]{1,0:T(2,128)S(1)}, s32[]{:T(128)}, bf16[2,4096,1,128]{3,1,0,2:T(8,128)(2,1)}, ...), branch_computations={%region_7.9_spmd, %region_10.10_spmd} | conditional | flops 551294976 | bytes 16898114 | solution.py:117
  303.0 2.7 fusion.9
  308.4 5.8 %conditional.2 = (f32[2,1,4,256]{3,2,0,1:T(4,128)S(1)}, f32[2,1,4,256]{3,2,0,1:T(4,128)S(1)}, f32[2,1,4,256,128]{4,3,2,0,1:T(8,128)S(1)}) conditional(s32[]{:T(128)} %convert_element_type.120, (s32[2,512]{1,0:T(2,128)S(1)}, s32[2,256]{1,0:T(2,128)S(1)}, s32[]{:T(128)}, bf16[2,4096,1,128]{3,1,0,2:T(8,128)(2,1)}, ...), branch_computations={%region_7.9_spmd, %region_10.10_spmd} | conditional | flops 551294976 | bytes 16898114 | solution.py:117
  310.5 2.6 fusion.9
  315.9 5.8 %conditional.2 = (f32[2,1,4,256]{3,2,0,1:T(4,128)S(1)}, f32[2,1,4,256]{3,2,0,1:T(4,128)S(1)}, f32[2,1,4,256,128]{4,3,2,0,1:T(8,128)S(1)}) conditional(s32[]{:T(128)} %convert_element_type.120, (s32[2,512]{1,0:T(2,128)S(1)}, s32[2,256]{1,0:T(2,128)S(1)}, s32[]{:T(128)}, bf16[2,4096,1,128]{3,1,0,2:T(8,128)(2,1)}, ...), branch_computations={%region_7.9_spmd, %region_10.10_spmd} | conditional | flops 551294976 | bytes 16898114 | solution.py:117
  317.9 2.6 fusion.9
  322.4 10.1 %convolution_convert_fusion = bf16[512,8192]{1,0:T(8,128)(2,1)} fusion(bf16[512,8192]{1,0:T(8,128)(2,1)} %all-gather.11.cloned.1.call-done, bf16[64,8,4,128]{3,2,1,0:T(4,128)(2,1)S(1)} %bitcast.93), kind=kOutput, calls=%fused_computation.44 | convolution fusion | flops 4299161600 | bytes 17301504 | tf_op jit(solution)/shard_map/dot_general | solution.py:124
  332.6 114.6 %reduce-scatter.2.cloned.1.call-done = bf16[512,1024]{1,0:T(8,128)(2,1)} async-done(((bf16[512,8192]{1,0:T(8,128)(2,1)}), bf16[512,1024]{1,0:T(8,128)(2,1)}) %reduce-scatter.2.cloned.1.call-update) | async-done | bytes 1048592 | tf_op jit(solution)/shard_map/reduce_scatter | solution.py:129
  (123 shorter events, 37.7 us)
Async XLA Ops:
  6.5 5.1 %copy-start = (s32[2,32]{1,0:T(2,128)S(1)}, s32[2,32]{1,0:T(2,128)}, u32[]{:S(2)}) copy-start(s32[2,32]{1,0:T(2,128)} %param.13) | copy-start | bytes 772
  6.5 112.1 %all-gather.5.cloned.1.call-start = ((), (), s32[]{:S(2)}) async-start(), calls=%async_computation.1 | async-start | bytes 9437184 | tf_op jit(solution)/shard_map/all_gather | solution.py:59
  7.3 182.8 %all-gather.7.cloned.1.call-start = ((), (), s32[]{:S(2)}) async-start(), calls=%async_computation.2 | async-start | bytes 13369344 | tf_op jit(solution)/shard_map/all_gather | solution.py:19
  11.5 240.1 %all-gather.9.cloned.1.call-start = ((), (), s32[]{:S(2)}) async-start(), calls=%async_computation.3 | async-start | bytes 4456448 | tf_op jit(solution)/shard_map/all_gather | solution.py:19
  11.8 178.3 %copy-start.1 = (f32[8192]{0:T(1024)S(1)}, f32[8192]{0:T(1024)}, u32[]{:S(2)}) copy-start(f32[8192]{0:T(1024)} %param.12) | copy-start | bytes 98308
  205.4 117.0 %all-gather.11.cloned.1.call-start = ((), (), s32[]{:S(2)}) async-start(), calls=%async_computation.4 | async-start | bytes 8912896 | tf_op jit(solution)/shard_map/all_gather | solution.py:126
  206.0 241.2 %reduce-scatter.2.cloned.1.call-start = ((), (), s32[]{:S(2)}) async-start(), calls=%async_computation.5 | async-start | bytes 9437184 | tf_op jit(solution)/shard_map/reduce_scatter | solution.py:129
Sparse Core Ops, SparseCore 0:
  9.6 108.9 all-gather.4
  120.3 69.7 all-gather.6
  205.5 46.0 all-gather.8
  253.1 52.2 all-gather.10
  332.7 114.4 reduce-scatter.1
where the time goes:
time: 455 us; the launch traced here: 454 us
  waiting for transfers between devices  316 us (69%)
  matrix products  69.2 us (15%)
  other arithmetic  26.5 us (6%)
  local copies, waits for them, and re-layouts  22.2 us (5%)
  between operations  13.3 us (3%)
  loops' own time  6.33 us (1%)
    reduce_scatter x1, waiting for transfers between devices, per_device(): lax.psum_scatter(terms.astype(jnp.bfloat16), 'tp', scatter_dimension=1, t...  115 us
    all_gather x1, waiting for transfers between devices, per_device(): whole = lax.all_gather(tokens, 'tp', axis=2, tiled=True)  107 us
    all_gather x2, waiting for transfers between devices, in_one_piece(): lax.all_gather(both, axis, axis=dim, tiled=True)  93.1 us
    dot_general x3, matrix products, per_device(): jnp.dot(normed, piece, preferred_element_type=jnp.float32)  23.8 us
    dot_general x8, matrix products, update(): jnp.einsum('shgqk,skhd->shgqd', weights.astype(jnp.bfloat16), value_block...  21.2 us
    dot_general x8, matrix products, update(): jnp.einsum('shgqd,skhd->shgqk', query, key_block, preferred_element_type=...  14.2 us
    split x2, local copies, waits for them, and re-layouts, in_one_piece(): jnp.split(lax.all_gather(both, axis, axis=dim, tiled=True), ends, axis=al...  11.6 us
    dot_general x1, matrix products, per_device(): jnp.dot(attended, lax.all_gather(w_out, 'ctx', axis=1, tiled=True), prefe...  10.1 us
  transfers between devices with their start and end apart: 5, of which 4 were waited for; matrix products, arithmetic and copies ran while one was open for 20% of the time, Pallas kernels for 0%

commit v1 on v0

--- a/solution.py
+++ b/solution.py
@@ -56,7 +56,7 @@
     total_rows = sequence_batch * rows_dev
     factor = 1.0 / math.sqrt(head_size)
     rank = lax.axis_index("ctx")
-    whole = lax.all_gather(tokens, "tp", axis=2, tiled=True)
+    whole = jnp.concatenate(lax.all_gather(tokens, "tp"), axis=2)
     normed = normalize(whole.reshape(total_rows, whole.shape[2]), norm_gain)
     query_pos = positions_of(span_order, rank * rows_dev, rows_dev, block_rows)
     latest = jnp.max(query_pos, axis=1)

time: 455 us -> 464 us (1.020)
  waiting for transfers between devices: 316 us -> 269 us
  local copies, waits for them, and re-layouts: 22.2 us -> 60.4 us
  other arithmetic: 26.5 us -> 44.6 us
    all_gather x2, waiting for transfers between devices: 93.1 us -> 45.8 us  [in_one_piece(): lax.all_gather(both, axis, axis=dim, tiled=True)]
    convert_element_type x0 -> x2, local copies, waits for them, and re-layouts: none -> 25.7 us  [the longest x1 13.6 us: normalize(): return (wide * factor * norm_gain).astype(jnp.bfloat16)]
    unnamed x0 -> x2, other arithmetic: none -> 11.8 us
    mul x0 -> x2, local copies, waits for them, and re-layouts: none -> 11.3 us  [normalize(): return (wide * factor * norm_gain).astype(jnp.bfloat16)]
    mul x0 -> x1, other arithmetic: none -> 9.42 us  [normalize(): return (wide * factor * norm_gain).astype(jnp.bfloat16)]
  transfers between devices with their start and end apart: 5 -> 5, of which waited for: 4 -> 3; matrix products, arithmetic and copies ran while one was open for 20% -> 32% of each run, Pallas kernels for 0% -> 0%
where the time goes in v1:
time: 464 us; the launch traced here: 463 us
  waiting for transfers between devices  269 us (58%)
  matrix products  69.3 us (15%)
  local copies, waits for them, and re-layouts  60.4 us (13%)
  other arithmetic  44.6 us (10%)
  between operations  13.3 us (3%)
  loops' own time  5.96 us (1%)
    reduce_scatter x1, waiting for transfers between devices, per_device(): lax.psum_scatter(terms.astype(jnp.bfloat16), 'tp', scatter_dimension=1, t...  115 us
    all_gather x1, waiting for transfers between devices, per_device(): whole = jnp.concatenate(lax.all_gather(tokens, 'tp'), axis=2)  106 us
    all_gather x2, waiting for transfers between devices, in_one_piece(): lax.all_gather(both, axis, axis=dim, tiled=True)  45.8 us
    dot_general x3, matrix products, per_device(): jnp.dot(normed, piece, preferred_element_type=jnp.float32)  23.8 us
    dot_general x8, matrix products, update(): jnp.einsum('shgqk,skhd->shgqd', weights.astype(jnp.bfloat16), value_block...  21.2 us
    dot_general x8, matrix products, update(): jnp.einsum('shgqd,skhd->shgqk', query, key_block, preferred_element_type=...  14.2 us
    convert_element_type x1, local copies, waits for them, and re-layouts, normalize(): return (wide * factor * norm_gain).astype(jnp.bfloat16)  13.6 us
    convert_element_type x1, local copies, waits for them, and re-layouts, normalize(): wide = flat_rows.astype(jnp.float32)  12.1 us
  transfers between devices with their start and end apart: 5, of which 3 were waited for; matrix products, arithmetic and copies ran while one was open for 32% of the time, Pallas kernels for 0%

profile of v1, /device:TPU:0, one launch (start us, length us, event | category | flops | bytes accessed | tf_op | source)
XLA Modules:
  0.0 462.5 jit_solution(10028210709312620511)
XLA Ops:
  12.4 106.2 %all-gather.12.cloned.1.call-done = bf16[16,256,1024]{2,1,0:T(8,128)(2,1)} async-done(((bf16[2,256,1024]{2,1,0:T(8,128)(2,1)}), bf16[16,256,1024]{2,1,0:T(8,128)(2,1)}) %all-gather.12.cloned.1.call-update) | async-done | bytes 8388624 | tf_op jit(solution)/shard_map/all_gather | solution.py:59
  118.7 11.8 %convert_bitcast_fusion = f32[8,2,32,8,1024]{4,3,2,1,0:T(8,128)} fusion(bf16[16,256,1024]{2,1,0:T(8,128)(2,1)} %all-gather.12.cloned.1.call-done), kind=kLoop, calls=%fused_computation.41 | loop fusion | flops 4194304 | bytes 25165824
  130.4 12.1 %copy.62 = f32[8,2,32,8,1024]{4,3,0,2,1:T(8,128)} copy(f32[8,2,32,8,1024]{4,3,2,1,0:T(8,128)} %convert_bitcast_fusion) | data formatting | bytes 33554432 | tf_op jit(solution)/shard_map/convert_element_type | solution.py:23
  144.3 45.8 %all-gather.6.cloned.1.call-done = bf16[8192,768]{0,1:T(8,128)(2,1)} async-done(((bf16[512,768]{0,1:T(8,128)(2,1)}), bf16[8192,768]{0,1:T(8,128)(2,1)}) %all-gather.6.cloned.1.call-update) | async-done | bytes 12582928 | tf_op jit(solution)/shard_map/all_gather | solution.py:19
  190.1 9.5 %fusion.35 = f32[2,256,1,128]{1,3,0,2:T(8,128)S(1)} fusion(bf16[8192,768]{0,1:T(8,128)(2,1)} %all-gather.6.cloned.1.call-done, f32[2,256,8192]{2,1,0:T(8,128)} %bitcast.100, f32[8192]{0:T(1024)S(1)} %copy-done.1, f32[2,256]{1,0:T(2,128)S(1)} %add_rsqrt_fusion), kind=kOutput, calls=%fused_computation.54 | convolution fusion | flops 1086324736 | bytes 19171328 | tf_op jit(solution)/shard_map/dot_general | solution.py:71
  201.2 4.8 %fusion.37 = bf16[2,256,1,128]{1,3,0,2:T(8,128)(2,1)S(1)} fusion(bf16[8192,768]{0,1:T(8,128)(2,1)} %all-gather.6.cloned.1.call-done, f32[2,256,8192]{2,1,0:T(8,128)S(1)} %bitcast.101, f32[8192]{0:T(1024)S(1)} %copy-done.1, f32[2,256]{1,0:T(2,128)S(1)} %add_rsqrt_fusion), kind=kOutput, calls=%fused_computation.56 | convolution fusion | flops 1086390272 | bytes 19040256 | tf_op jit(solution)/shard_map/dot_general | solution.py:71
  208.2 9.4 %fusion.30 = bf16[2,256,8,1024]{3,1,0,2:T(8,128)(2,1)} fusion(f32[8,1024]{1,0:T(8,128)S(1)} %mul.228, f32[2,256]{1,0:T(2,128)S(1)} %add_rsqrt_fusion, bf16[16,256,1024]{2,1,0:T(8,128)(2,1)} %all-gather.12.cloned.1.call-done), kind=kLoop, calls=%fused_computation.47 | loop fusion | flops 16777216 | bytes 16812032 | tf_op jit(solution)/shard_map/mul | solution.py:25
  217.6 11.3 %copy.50 = bf16[2,256,8,1024]{3,2,1,0:T(8,128)(2,1)} copy(bf16[2,256,8,1024]{3,1,0,2:T(8,128)(2,1)} %fusion.30) | data formatting | bytes 16777216 | tf_op jit(solution)/shard_map/mul | solution.py:25
  229.0 13.6 %reshape.362 = bf16[2,256,8192,1]{2,1,0,3:T(8,128)(2,1)} reshape(bf16[2,256,8,1024]{3,2,1,0:T(8,128)(2,1)} %copy.50) | data formatting | bytes 16777216 | tf_op jit(solution)/shard_map/convert_element_type | solution.py:25
  242.6 7.8 %split.23 = bf16[8192,512]{0,1:T(8,128)(2,1)} slice(bf16[8192,768]{0,1:T(8,128)(2,1)} %all-gather.6.cloned.1.call-done), slice={[0:8192], [0:512]} | slice | bytes 16777216 | tf_op jit(solution)/shard_map/split | solution.py:19
  250.4 9.5 %fusion.31 = f32[2,256,4,128]{1,3,2,0:T(8,128)S(1)} fusion(bf16[4,128,8192,1]{2,1,0,3:T(8,128)(2,1)} %bitcast.105, bf16[2,256,8192,1]{2,1,0,3:T(8,128)(2,1)} %reshape.362), kind=kOutput, calls=%fused_computation.48 | convolution fusion | flops 4294967296 | bytes 17825792 | tf_op jit(solution)/shard_map/dot_general | solution.py:71
  260.4 3.9 fusion.54
  264.4 4.1 copy.51
  271.0 58.9 %while.19 = (s32[]{:T(128)}, f32[2,1,4,256]{3,2,0,1:T(4,128)S(1)}, f32[2,1,4,256]{3,2,0,1:T(4,128)S(1)}, f32[2,1,4,256,128]{4,3,2,0,1:T(8,128)S(1)}, s32[2,32]{1...) while((s32[]{:T(128)}, f32[2,1,4,256]{3,2,0,1:T(4,128)S(1)}, ...), condition=%wide.region_11.12_spmd, body=%wide.region_3.11_spmd.sunk | while | flops 551389184 | bytes 16968260 | solution.py:121
  272.6 5.8 %conditional.2 = (f32[2,1,4,256]{3,2,0,1:T(4,128)S(1)}, f32[2,1,4,256]{3,2,0,1:T(4,128)S(1)}, f32[2,1,4,256,128]{4,3,2,0,1:T(8,128)S(1)}) conditional(s32[]{:T(128)} %convert_element_type.129, (s32[2,512]{1,0:T(2,128)S(1)}, s32[2,256]{1,0:T(2,128)S(1)}, s32[]{:T(128)}, bf16[2,4096,1,128]{3,1,0,2:T(8,128)(2,1)}, ...), branch_computations={%region_7.9_spmd, %region_10.10_spmd} | conditional | flops 551294976 | bytes 16898114 | solution.py:117
  274.6 2.6 fusion.9
  279.9 5.8 %conditional.2 = (f32[2,1,4,256]{3,2,0,1:T(4,128)S(1)}, f32[2,1,4,256]{3,2,0,1:T(4,128)S(1)}, f32[2,1,4,256,128]{4,3,2,0,1:T(8,128)S(1)}) conditional(s32[]{:T(128)} %convert_element_type.129, (s32[2,512]{1,0:T(2,128)S(1)}, s32[2,256]{1,0:T(2,128)S(1)}, s32[]{:T(128)}, bf16[2,4096,1,128]{3,1,0,2:T(8,128)(2,1)}, ...), branch_computations={%region_7.9_spmd, %region_10.10_spmd} | conditional | flops 551294976 | bytes 16898114 | solution.py:117
  281.9 2.7 fusion.9
  287.3 5.8 %conditional.2 = (f32[2,1,4,256]{3,2,0,1:T(4,128)S(1)}, f32[2,1,4,256]{3,2,0,1:T(4,128)S(1)}, f32[2,1,4,256,128]{4,3,2,0,1:T(8,128)S(1)}) conditional(s32[]{:T(128)} %convert_element_type.129, (s32[2,512]{1,0:T(2,128)S(1)}, s32[2,256]{1,0:T(2,128)S(1)}, s32[]{:T(128)}, bf16[2,4096,1,128]{3,1,0,2:T(8,128)(2,1)}, ...), branch_computations={%region_7.9_spmd, %region_10.10_spmd} | conditional | flops 551294976 | bytes 16898114 | solution.py:117
  289.4 2.6 fusion.9
  294.7 5.8 %conditional.2 = (f32[2,1,4,256]{3,2,0,1:T(4,128)S(1)}, f32[2,1,4,256]{3,2,0,1:T(4,128)S(1)}, f32[2,1,4,256,128]{4,3,2,0,1:T(8,128)S(1)}) conditional(s32[]{:T(128)} %convert_element_type.129, (s32[2,512]{1,0:T(2,128)S(1)}, s32[2,256]{1,0:T(2,128)S(1)}, s32[]{:T(128)}, bf16[2,4096,1,128]{3,1,0,2:T(8,128)(2,1)}, ...), branch_computations={%region_7.9_spmd, %region_10.10_spmd} | conditional | flops 551294976 | bytes 16898114 | solution.py:117
  296.7 2.6 fusion.9
  302.1 5.7 %conditional.2 = (f32[2,1,4,256]{3,2,0,1:T(4,128)S(1)}, f32[2,1,4,256]{3,2,0,1:T(4,128)S(1)}, f32[2,1,4,256,128]{4,3,2,0,1:T(8,128)S(1)}) conditional(s32[]{:T(128)} %convert_element_type.129, (s32[2,512]{1,0:T(2,128)S(1)}, s32[2,256]{1,0:T(2,128)S(1)}, s32[]{:T(128)}, bf16[2,4096,1,128]{3,1,0,2:T(8,128)(2,1)}, ...), branch_computations={%region_7.9_spmd, %region_10.10_spmd} | conditional | flops 551294976 | bytes 16898114 | solution.py:117
  304.1 2.6 fusion.9
  309.4 5.7 %conditional.2 = (f32[2,1,4,256]{3,2,0,1:T(4,128)S(1)}, f32[2,1,4,256]{3,2,0,1:T(4,128)S(1)}, f32[2,1,4,256,128]{4,3,2,0,1:T(8,128)S(1)}) conditional(s32[]{:T(128)} %convert_element_type.129, (s32[2,512]{1,0:T(2,128)S(1)}, s32[2,256]{1,0:T(2,128)S(1)}, s32[]{:T(128)}, bf16[2,4096,1,128]{3,1,0,2:T(8,128)(2,1)}, ...), branch_computations={%region_7.9_spmd, %region_10.10_spmd} | conditional | flops 551294976 | bytes 16898114 | solution.py:117
  311.4 2.6 fusion.9
  316.7 5.7 %conditional.2 = (f32[2,1,4,256]{3,2,0,1:T(4,128)S(1)}, f32[2,1,4,256]{3,2,0,1:T(4,128)S(1)}, f32[2,1,4,256,128]{4,3,2,0,1:T(8,128)S(1)}) conditional(s32[]{:T(128)} %convert_element_type.129, (s32[2,512]{1,0:T(2,128)S(1)}, s32[2,256]{1,0:T(2,128)S(1)}, s32[]{:T(128)}, bf16[2,4096,1,128]{3,1,0,2:T(8,128)(2,1)}, ...), branch_computations={%region_7.9_spmd, %region_10.10_spmd} | conditional | flops 551294976 | bytes 16898114 | solution.py:117
  318.8 2.6 fusion.9
  324.1 5.7 %conditional.2 = (f32[2,1,4,256]{3,2,0,1:T(4,128)S(1)}, f32[2,1,4,256]{3,2,0,1:T(4,128)S(1)}, f32[2,1,4,256,128]{4,3,2,0,1:T(8,128)S(1)}) conditional(s32[]{:T(128)} %convert_element_type.129, (s32[2,512]{1,0:T(2,128)S(1)}, s32[2,256]{1,0:T(2,128)S(1)}, s32[]{:T(128)}, bf16[2,4096,1,128]{3,1,0,2:T(8,128)(2,1)}, ...), branch_computations={%region_7.9_spmd, %region_10.10_spmd} | conditional | flops 551294976 | bytes 16898114 | solution.py:117
  326.1 2.6 fusion.9
  330.7 10.1 %convolution_convert_fusion = bf16[512,8192]{1,0:T(8,128)(2,1)} fusion(bf16[512,8192]{1,0:T(8,128)(2,1)} %all-gather.10.cloned.1.call-done, bf16[64,8,4,128]{3,2,1,0:T(4,128)(2,1)S(1)} %bitcast.108), kind=kOutput, calls=%fused_computation.46 | convolution fusion | flops 4299161600 | bytes 17301504 | tf_op jit(solution)/shard_map/dot_general | solution.py:124
  340.7 115.3 %reduce-scatter.2.cloned.1.call-done = bf16[512,1024]{1,0:T(8,128)(2,1)} async-done(((bf16[512,8192]{1,0:T(8,128)(2,1)}), bf16[512,1024]{1,0:T(8,128)(2,1)}) %reduce-scatter.2.cloned.1.call-update) | async-done | bytes 1048592 | tf_op jit(solution)/shard_map/reduce_scatter | solution.py:129
  (136 shorter events, 46.9 us)
Async XLA Ops:
  6.5 112.1 %all-gather.12.cloned.1.call-start = ((), (), s32[]{:S(2)}) async-start(), calls=%async_computation.5 | async-start | bytes 9437184 | tf_op jit(solution)/shard_map/all_gather | solution.py:59
  7.3 182.8 %all-gather.6.cloned.1.call-start = ((), (), s32[]{:S(2)}) async-start(), calls=%async_computation.1 | async-start | bytes 13369344 | tf_op jit(solution)/shard_map/all_gather | solution.py:19
  11.5 248.9 %all-gather.8.cloned.1.call-start = ((), (), s32[]{:S(2)}) async-start(), calls=%async_computation.2 | async-start | bytes 4456448 | tf_op jit(solution)/shard_map/all_gather | solution.py:19
  118.7 23.9 %slice-start = ((s8[8388608]{0:T(1024)(128)(4,1)}), s8[4194304]{0:T(1024)(128)(4,1)S(1)}, s32[]{:S(2)}) async-start(s8[8388608]{0:T(1024)(128)(4,1)} %bitcast.102), calls=%async_computation.6 | async-start | bytes 8388608
  130.4 12.1 %slice-start.1 = ((s8[8388608]{0:T(1024)(128)(4,1)}), s8[4194304]{0:T(1024)(128)(4,1)S(1)}, s32[]{:S(2)}) async-start(s8[8388608]{0:T(1024)(128)(4,1)} %bitcast.102), calls=%async_computation.7 | async-start | bytes 8388608
  142.5 47.6 %copy-start.1 = (f32[8192]{0:T(1024)S(1)}, f32[8192]{0:T(1024)}, u32[]{:S(2)}) copy-start(f32[8192]{0:T(1024)} %param.12) | copy-start | bytes 98308
  190.1 11.1 %copy-start = (f32[8,2,32,8,1024]{4,3,0,2,1:T(8,128)S(1)}, f32[8,2,32,8,1024]{4,3,0,2,1:T(8,128)}, u32[]{:S(2)}) copy-start(f32[8,2,32,8,1024]{4,3,0,2,1:T(8,128)} %copy.62) | copy-start | bytes 50331652
  206.7 123.9 %all-gather.10.cloned.1.call-start = ((), (), s32[]{:S(2)}) async-start(), calls=%async_computation.3 | async-start | bytes 8912896 | tf_op jit(solution)/shard_map/all_gather | solution.py:126
  207.3 248.7 %reduce-scatter.2.cloned.1.call-start = ((), (), s32[]{:S(2)}) async-start(), calls=%async_computation.4 | async-start | bytes 9437184 | tf_op jit(solution)/shard_map/reduce_scatter | solution.py:129
  260.4 10.6 %copy-start.2 = (s32[2,32]{1,0:T(2,128)S(1)}, s32[2,32]{1,0:T(2,128)}, u32[]{:S(2)}) copy-start(s32[2,32]{1,0:T(2,128)} %param.13) | copy-start | bytes 772
Sparse Core Ops, SparseCore 0:
  9.7 108.9 all-gather.11
  120.3 69.7 all-gather.5
  206.9 46.0 all-gather.7
  254.5 52.2 all-gather.9
  340.9 115.0 reduce-scatter.1
